TPU v7x, 32 devices: a whole 2x2x4 slice. The times are simulated.
32 devices in a mesh: fsdp: 16 (over z, y, core), grp: 2 (over x).
Axes of the slice: x: 2, y: 2, z: 4, core: 2. Of those that a mesh axis runs over, the one named last changes fastest.
Arguments:
- hidden: bfloat16 [8192, 3072], P('fsdp', 'grp'), may hold values from -16 to 16
- queries: bfloat16 [8192, 1536], P('fsdp', 'grp'), may hold values from -6 to 6
- attn_keys: bfloat16 [8192, 1536], P('fsdp', 'grp'), may hold values from -6 to 6
- w_value: bfloat16 [1536, 3072], P('fsdp', 'grp'), may hold values from -1 to 1
- w_out: bfloat16 [1536, 3072], P('fsdp', 'grp'), may hold values from -1 to 1
- alpha: float32 [3072], P('grp'), may hold values from 0.05 to 0.5
- out_grad: bfloat16 [8192, 3072], P('fsdp', 'grp'), may hold values from -6 to 6
Outputs:
- new_hidden: bfloat16 [8192, 3072], P('fsdp', 'grp')
- grad_hidden: bfloat16 [8192, 3072], P('fsdp', 'grp')
- grad_queries: bfloat16 [8192, 1536], P('fsdp', 'grp')
- grad_keys: bfloat16 [8192, 1536], P('fsdp', 'grp')
- grad_w_value: float32 [1536, 3072], P('fsdp', 'grp')
- grad_w_out: float32 [1536, 3072], P('fsdp', 'grp')
All inputs are finite; a program needn't handle non-finite values.
Results may differ from a plain program's by a relative error of at most 0.012.
The roundings to bfloat16 on the way count: a program that leaves them out, or rounds other values in their place, can miss the bound.
Values may be sent and summed in bfloat16 or wider, within the bound.
A program may use at most 192 MiB of HBM per device.

v0:
```python
import jax
import jax.numpy as jnp
from jax import lax
from jax.sharding import PartitionSpec as P

D = 3072
HS = 128


EPS = 1e-06


def contract_last(left, right):
    return lax.dot_general(
        left, right, (((1,), (1,)), ((), ())), preferred_element_type=jnp.float32
    )


def contract_first(left, right):
    return lax.dot_general(
        left, right, (((0,), (0,)), ((), ())), preferred_element_type=jnp.float32
    )


def causal_probs(query_head, key_head):
    length = query_head.shape[0]
    score_scale = query_head.shape[1] ** (-0.5)
    scores = contract_last(query_head, key_head) * score_scale
    row_pos = lax.broadcasted_iota(jnp.int32, (length, length), 0)
    col_pos = lax.broadcasted_iota(jnp.int32, (length, length), 1)
    scores = jnp.where(row_pos >= col_pos, scores, -1e30)
    row_peak = jnp.max(scores, axis=1, keepdims=True)
    exp_terms = jnp.exp(scores - row_peak)
    return exp_terms / jnp.sum(exp_terms, axis=1, keepdims=True)


def head_forward(items):
    query_head, key_head, value_head = items
    attn_prob = causal_probs(query_head, key_head)
    return jnp.dot(
        attn_prob.astype(jnp.bfloat16), value_head, preferred_element_type=jnp.float32
    ).astype(jnp.bfloat16)


def head_backward(items):
    query_head, key_head, value_head, grad_head = items
    score_scale = query_head.shape[1] ** (-0.5)
    attn_prob = causal_probs(query_head, key_head)
    prob_half = attn_prob.astype(jnp.bfloat16)
    grad_prob = contract_last(grad_head, value_head)
    row_delta = jnp.sum(attn_prob * grad_prob, axis=1, keepdims=True)
    grad_score = (attn_prob * (grad_prob - row_delta)).astype(jnp.bfloat16)
    grad_query = (
        jnp.dot(grad_score, key_head, preferred_element_type=jnp.float32) * score_scale
    ).astype(jnp.bfloat16)
    grad_key = (contract_first(grad_score, query_head) * score_scale).astype(jnp.bfloat16)
    grad_value = contract_first(prob_half, grad_head).astype(jnp.bfloat16)
    return (grad_query, grad_key, grad_value)


def split_heads(block):
    return block.reshape(block.shape[0], -1, HS).transpose(1, 0, 2)


def join_heads(stacked):
    return stacked.transpose(1, 0, 2).reshape(stacked.shape[1], -1)


def shards(hidden, queries, attn_keys, w_value, w_out, alpha, out_grad):
    half_width = hidden.shape[1]
    value_rows = w_value.astype(jnp.float32)
    out_rows = w_out.astype(jnp.float32)
    row_sums = lax.psum(
        (jnp.sum(value_rows * value_rows, axis=1), jnp.sum(out_rows * out_rows, axis=1)), "grp"
    )
    norm_v = jnp.sqrt(row_sums[0] + EPS)[:, None]
    norm_o = jnp.sqrt(row_sums[1] + EPS)[:, None]
    unit_v = value_rows / norm_v
    unit_o = out_rows / norm_o
    weight_v, weight_o = (
        lax.all_gather(unit_v.astype(jnp.bfloat16), "fsdp", axis=0, tiled=True),
        lax.all_gather(unit_o.astype(jnp.bfloat16), "fsdp", axis=0, tiled=True),
    )
    value_parts = contract_last(hidden, weight_v)
    values_mine = lax.psum_scatter(value_parts, "grp", scatter_dimension=1, tiled=True).astype(
        jnp.bfloat16
    )
    q_heads = split_heads(queries)
    k_heads = split_heads(attn_keys)
    v_heads = split_heads(values_mine)
    attn_mine = join_heads(lax.map(head_forward, (q_heads, k_heads, v_heads)))
    attn_all = lax.all_gather(attn_mine, "grp", axis=1, tiled=True)
    proj = jnp.dot(attn_all, weight_o, preferred_element_type=jnp.float32)
    hidden_f = hidden.astype(jnp.float32)
    keep_rate = 1.0 - alpha
    moments = lax.psum(
        (
            jnp.sum(proj * proj, axis=1),
            jnp.sum(keep_rate * keep_rate * hidden_f * hidden_f, axis=1),
            jnp.sum(keep_rate * alpha * hidden_f * proj, axis=1),
            jnp.sum(alpha * alpha * proj * proj, axis=1),
        ),
        "grp",
    )
    proj_rs = lax.rsqrt(moments[0] / D + EPS)[:, None]
    cross_sum = moments[2][:, None]
    alpha_sum = moments[3][:, None]
    mix_mean = (moments[1][:, None] + 2.0 * proj_rs * cross_sum + proj_rs * proj_rs * alpha_sum) / D
    mix_rs = lax.rsqrt(mix_mean + EPS)
    mixed = hidden_f + alpha * (proj * proj_rs - hidden_f)
    new_hidden = (mixed * mix_rs).astype(jnp.bfloat16)
    grad_out = out_grad.astype(jnp.float32)
    grad_sums = lax.psum(
        (
            jnp.sum(grad_out * keep_rate * hidden_f, axis=1),
            jnp.sum(grad_out * alpha * proj, axis=1),
        ),
        "grp",
    )
    grad_mean = (grad_sums[0][:, None] + proj_rs * grad_sums[1][:, None]) / D
    grad_mix = mix_rs * (grad_out - mixed * mix_rs * mix_rs * grad_mean)
    grad_pn = grad_mix * alpha
    proj_mean = (
        mix_rs * grad_sums[1][:, None]
        - mix_rs * mix_rs * mix_rs * grad_mean * (cross_sum + proj_rs * alpha_sum)
    ) / D
    grad_res = grad_mix * keep_rate
    grad_proj = proj_rs * (grad_pn - proj * proj_rs * proj_rs * proj_mean)
    grad_proj_b = grad_proj.astype(jnp.bfloat16)
    grad_attn_parts = contract_last(grad_proj_b, weight_o)
    grad_attn = lax.psum_scatter(grad_attn_parts, "grp", scatter_dimension=1, tiled=True).astype(
        jnp.bfloat16
    )
    grad_q, grad_k, grad_v = lax.map(
        head_backward, (q_heads, k_heads, v_heads, split_heads(grad_attn))
    )
    grad_values = lax.all_gather(join_heads(grad_v), "grp", axis=1, tiled=True)
    grad_hidden = (
        grad_res + jnp.dot(grad_values, weight_v, preferred_element_type=jnp.float32)
    ).astype(jnp.bfloat16)
    owned = lax.psum_scatter(
        jnp.concatenate(
            (contract_first(grad_values, hidden), contract_first(attn_all, grad_proj_b)), axis=1
        ),
        "fsdp",
        scatter_dimension=0,
        tiled=True,
    )
    gw_v_own = owned[:, :half_width]
    gw_o_own = owned[:, half_width:]
    row_dot = lax.psum(
        (jnp.sum(gw_v_own * unit_v, axis=1), jnp.sum(gw_o_own * unit_o, axis=1)), "grp"
    )
    grad_w_value = (gw_v_own - unit_v * row_dot[0][:, None]) / norm_v
    grad_w_out = (gw_o_own - unit_o * row_dot[1][:, None]) / norm_o
    return (
        new_hidden,
        grad_hidden,
        join_heads(grad_q),
        join_heads(grad_k),
        grad_w_value,
        grad_w_out,
    )


def solution(mesh):
    placed = (
        P("fsdp", "grp"),
        P("fsdp", "grp"),
        P("fsdp", "grp"),
        P("fsdp", "grp"),
        P("fsdp", "grp"),
        P("grp"),
        P("fsdp", "grp"),
    )
    return jax.shard_map(
        shards,
        mesh=mesh,
        in_specs=placed,
        out_specs=(
            P("fsdp", "grp"),
            P("fsdp", "grp"),
            P("fsdp", "grp"),
            P("fsdp", "grp"),
            P("fsdp", "grp"),
            P("fsdp", "grp"),
        ),
        check_vma=False,
    )
```

profile of v0, /device:TPU:0, one launch (start us, length us, event | category | flops | bytes accessed | tf_op | source)
XLA Modules:
  0.0 593.8 jit_solution(14473532207321060292)
XLA Ops:
  7.2 1.3 fusion.52
  8.5 5.9 all-reduce.2
  14.4 1.8 fusion.60
  16.2 55.0 %all-gather.5.cloned.1.call-done = bf16[1536,1536]{1,0:T(8,128)(2,1)} async-done(((bf16[96,1536]{1,0:T(8,128)(2,1)}), bf16[1536,1536]{1,0:T(8,128)(2,1)}) %all-gather.5.cloned.1.call-update) | async-done | bytes 4718608 | tf_op jit(solution)/shard_map/all_gather | solution.py:81
  71.3 7.1 %convolution_bitcast_fusion = f32[512,1536]{0,1:T(8,128)} fusion(bf16[1536,1536]{1,0:T(8,128)(2,1)} %all-gather.5.cloned.1.call-done, bf16[512,1536]{1,0:T(8,128)(2,1)} %param.11), kind=kOutput, calls=%fused_computation.68 | convolution fusion | flops 2415919104 | bytes 9437184 | tf_op jit(solution)/shard_map/dot_general | solution.py:14
  81.6 39.0 %reduce-scatter.6.cloned.1.call-done = f32[512,768]{0,1:T(8,128)} async-done(((f32[512,1536]{0,1:T(8,128)}), f32[512,768]{0,1:T(8,128)}) %reduce-scatter.6.cloned.1.call-update) | async-done | bytes 1572880 | tf_op jit(solution)/shard_map/reduce_scatter | solution.py:85
  120.6 1.5 convert_element_type.57
  123.3 11.8 %while.24 = (s32[]{:T(128)}, bf16[6,512,128]{1,2,0:T(8,128)(2,1)S(1)}, bf16[6,512,128]{2,1,0:T(8,128)(2,1)S(1)}, bf16[6,512,128]{2,1,0:T(8,128)(2,1)S(1)}, bf16[6,512,128]{2,1,0:T(8,128)(2,1)}, /*index=5*/s32[]{:T(128)}) while((s32[]{:T(128)}, bf16[6,512,128]{1,2,0:T(8,128)(2,1)S(1)}, bf16[6,512,128]{2,1,0:T(8,128)(2,1)S(1)}, ...), condition=%wide.region_6.7_spmd, body=%wide.region_3.6_spmd.sunk | while | flops 136641536 | bytes 4205653 | solution.py:91
  123.8 1.3 fusion.100
  125.8 1.3 fusion.100
  127.8 1.3 fusion.100
  129.7 1.3 fusion.100
  131.7 1.3 fusion.100
  133.7 1.3 fusion.100
  136.1 40.5 %all-gather.9.cloned.1.call-done = bf16[1536,1536]{1,0:T(8,128)(2,1)} async-done(((bf16[96,1536]{1,0:T(8,128)(2,1)}), bf16[1536,1536]{1,0:T(8,128)(2,1)}) %all-gather.9.cloned.1.call-update) | async-done | bytes 4718608 | tf_op jit(solution)/shard_map/all_gather | solution.py:82
  176.6 27.7 %all-gather.7.cloned.1.call-done = bf16[512,1536]{0,1:T(8,128)(2,1)} async-done(((bf16[512,768]{0,1:T(8,128)(2,1)}), bf16[512,1536]{0,1:T(8,128)(2,1)}) %all-gather.7.cloned.1.call-update) | async-done | bytes 1572880 | tf_op jit(solution)/shard_map/all_gather | solution.py:92
  204.3 8.4 %fusion.43 = (f32[512]{0:T(512)S(1)}, f32[512]{0:T(512)S(1)}, f32[512]{0:T(512)S(1)}, f32[512]{0:T(512)S(1)}, f32[512]{0:T(512)S(1)}, /*index=5*/f32[512]{0:T(512)S(1)}, f32[512,1536]{1,0:T(8,128)S(1)}) fusion(bf16[512,1536]{1,0:T(8,128)(2,1)} %param.17, f32[1536]{0:T(1024)S(1)} %copy-done.14, f32[1536]{0:T(1024)S(1)} %get-tuple-element.182, ...), kind=kOutput, calls=%fused_computation.72 | convolution fusion | flops 2430858240 | bytes 12625920 | tf_op jit(solution)/shard_map/dot_general | solution.py:93
  212.7 6.9 %all-reduce.1 = (f32[512]{0:T(512)S(1)}, f32[512]{0:T(512)S(1)}, f32[512]{0:T(512)S(1)}, f32[512]{0:T(512)S(1)}, f32[512]{0:T(512)S(1)}, /*index=5*/f32[512]{0:T(512)S(1)}) all-reduce(f32[512]{0:T(512)S(1)} %get-tuple-element.126, f32[512]{0:T(512)S(1)} %get-tuple-element.130, ...), channel_id=1, replica_groups=mesh['fsdp'=16,'grp'=2] {'grp'}, use_global_device_ids=true, to_apply=%region_16.17 | all-reduce | flops 3072 | bytes 24576 | tf_op jit(solution)/shard_map/psum | solution.py:96
  219.7 4.5 multiply_convert_fusion.1
  225.4 4.3 fusion.65
  229.7 44.7 %reduce-scatter.8.cloned.1.call-done = f32[512,768]{1,0:T(8,128)} async-done(((f32[512,1536]{1,0:T(8,128)}), f32[512,768]{1,0:T(8,128)}) %reduce-scatter.8.cloned.1.call-update) | async-done | bytes 1572880 | tf_op jit(solution)/shard_map/reduce_scatter | solution.py:131
  274.5 1.5 convert_element_type.63
  275.9 1.2 copy.46
  278.2 47.0 %while.25 = (s32[]{:T(128)}, bf16[6,512,128]{1,2,0:T(8,128)(2,1)}, bf16[6,512,128]{1,2,0:T(8,128)(2,1)S(1)}, bf16[6,512,128]{1,2,0:T(8,128)(2,1)S(1)}, bf16[6,51...) while((s32[]{:T(128)}, bf16[6,512,128]{1,2,0:T(8,128)(2,1)}, ...), condition=%wide.region_26.27_spmd, body=%wide.region_22.26_spmd.sunk | while | flops 340589056 | bytes 11821177 | solution.py:134
  278.2 1.3 fusion.107
  279.7 1.2 fusion.110
  281.0 1.3 multiply_reduce_fusion.5
  282.6 1.2 fusion.111
  283.8 1.3 fusion.109
  286.0 1.3 fusion.107
  287.5 1.2 fusion.110
  288.9 1.3 multiply_reduce_fusion.5
  290.5 1.2 fusion.111
  291.7 1.3 fusion.109
  293.9 1.3 fusion.107
  295.4 1.2 fusion.110
  296.7 1.3 multiply_reduce_fusion.5
  298.3 1.2 fusion.111
  299.5 1.3 fusion.109
  301.7 1.3 fusion.107
  303.2 1.2 fusion.110
  304.6 1.3 multiply_reduce_fusion.5
  306.1 1.2 fusion.111
  307.4 1.3 fusion.109
  309.6 1.3 fusion.107
  311.1 1.2 fusion.110
  312.4 1.3 multiply_reduce_fusion.5
  314.0 1.2 fusion.111
  315.2 1.3 fusion.109
  317.4 1.3 fusion.107
  318.9 1.2 fusion.110
  320.3 1.3 multiply_reduce_fusion.5
  321.8 1.2 fusion.111
  323.0 1.3 fusion.109
  326.2 8.5 %fusion.67 = f32[1536,1536]{0,1:T(8,128)} fusion(bf16[512,1536]{0,1:T(8,128)(2,1)} %all-gather.7.cloned.1.call-done, bf16[512,1536]{1,0:T(8,128)(2,1)} %copy-done.11), kind=kOutput, calls=%fused_computation.114 | convolution fusion | flops 2415919104 | bytes 12582912 | tf_op jit(solution)/shard_map/dot_general | solution.py:20
  334.7 18.8 %all-gather.11.cloned.1.call-done = bf16[512,1536]{0,1:T(8,128)(2,1)} async-done(((bf16[512,768]{0,1:T(8,128)(2,1)}), bf16[512,1536]{0,1:T(8,128)(2,1)}) %all-gather.11.cloned.1.call-update) | async-done | bytes 1572880 | tf_op jit(solution)/shard_map/all_gather | solution.py:137
  353.5 4.2 fusion.66
  357.8 7.2 %pad_maximum_fusion = f32[1536,3072]{0,1:T(8,128)} fusion(f32[1536,1536]{0,1:T(8,128)S(1)} %copy-done, f32[1536,1536]{0,1:T(8,128)S(1)} %fusion.66), kind=kLoop, calls=%fused_computation.57 | loop fusion | flops 4718592 | bytes 37748736 | tf_op jit(solution)/shard_map/concatenate | solution.py:142
  365.0 18.7 %copy.57 = f32[1536,3072]{1,0:T(8,128)} copy(f32[1536,3072]{0,1:T(8,128)} %pad_maximum_fusion) | data formatting | bytes 37748736
  387.1 9.9 %fusion.51 = bf16[512,1536]{1,0:T(8,128)(2,1)} fusion(bf16[512,1536]{0,1:T(8,128)(2,1)} %all-gather.11.cloned.1.call-done, bf16[1536,1536]{1,0:T(8,128)(2,1)} %all-gather.5.cloned.1.call-done, bf16[512,1536]{1,0:T(8,128)(2,1)S(1)} %copy-done.9, f32[512]{0:T(512)S(1)} %get-tuple-element.187, f32[1536]{0:T(1024)S(1)} %get-tuple-element.185, ...), kind=kOutput, calls=%fused_computation.82 | convolution fusion | flops 2426929152 | bytes 14174208 | tf_op jit(solution)/shard_map/dot_general | solution.py:139
  397.0 180.8 %reduce-scatter.10.cloned.1.call-done = f32[96,3072]{1,0:T(8,128)} async-done(((f32[1536,3072]{1,0:T(8,128)}), f32[96,3072]{1,0:T(8,128)}) %reduce-scatter.10.cloned.1.call-update) | async-done | bytes 1179664 | tf_op jit(solution)/shard_map/reduce_scatter | solution.py:141
  577.9 1.6 multiply_reduce_fusion.2
  579.5 4.9 all-reduce
  584.4 2.5 subtract_divide_fusion
  (128 shorter events, 25.0 us)
Async XLA Ops:
  7.2 64.1 %all-gather.5.cloned.1.call-start = ((), (), s32[]{:S(2)}) async-start(), calls=%async_computation.3 | async-start | bytes 5013504 | tf_op jit(solution)/shard_map/all_gather | solution.py:81
  16.2 104.4 %reduce-scatter.6.cloned.1.call-start = ((), (), s32[]{:S(2)}) async-start(), calls=%async_computation.4 | async-start | bytes 4718592 | tf_op jit(solution)/shard_map/reduce_scatter | solution.py:85
  78.4 1.0 copy-start.2
  78.4 1.9 copy-start.12
  78.4 2.5 copy-start.13
  78.4 98.1 %all-gather.9.cloned.1.call-start = ((), (), s32[]{:S(2)}) async-start(), calls=%async_computation.6 | async-start | bytes 5013504 | tf_op jit(solution)/shard_map/all_gather | solution.py:82
  80.2 124.1 %all-gather.7.cloned.1.call-start = ((), (), s32[]{:S(2)}) async-start(), calls=%async_computation.5 | async-start | bytes 2359296 | tf_op jit(solution)/shard_map/all_gather | solution.py:92
  123.3 12.8 %copy-start.14 = (f32[1536]{0:T(1024)S(1)}, f32[1536]{0:T(1024)}, u32[]{:S(2)}) copy-start(f32[1536]{0:T(1024)} %param.16) | copy-start | bytes 18436
  135.1 0.9 copy-start.5
  135.1 69.2 %copy-start.7 = (bf16[6,512,128]{2,1,0:T(8,128)(2,1)}, bf16[6,512,128]{2,1,0:T(8,128)(2,1)S(1)}, u32[]{:S(2)}) copy-start(bf16[6,512,128]{2,1,0:T(8,128)(2,1)S(1)} %get-tuple-element.351) | copy-start | bytes 2359300
  135.1 69.2 %copy-start.8 = (bf16[6,512,128]{2,1,0:T(8,128)(2,1)}, bf16[6,512,128]{2,1,0:T(8,128)(2,1)S(1)}, u32[]{:S(2)}) copy-start(bf16[6,512,128]{2,1,0:T(8,128)(2,1)S(1)} %get-tuple-element.352) | copy-start | bytes 2359300
  136.0 138.4 %reduce-scatter.8.cloned.1.call-start = ((), (), s32[]{:S(2)}) async-start(), calls=%async_computation.7 | async-start | bytes 4718592 | tf_op jit(solution)/shard_map/reduce_scatter | solution.py:131
  212.7 11.5 %copy-start.6 = (f32[512,1536]{1,0:T(8,128)}, f32[512,1536]{1,0:T(8,128)S(1)}, u32[]{:S(2)}) copy-start(f32[512,1536]{1,0:T(8,128)S(1)} %get-tuple-element.189) | copy-start | bytes 9437188
  219.7 5.7 copy-start.15
  224.2 1.1 copy-start.11
  229.7 123.8 %all-gather.11.cloned.1.call-start = ((), (), s32[]{:S(2)}) async-start(), calls=%async_computation.8 | async-start | bytes 2359296 | tf_op jit(solution)/shard_map/all_gather | solution.py:137
  325.3 0.9 copy-start.3
  326.2 27.4 %copy-start.10 = (bf16[512,1536]{1,0:T(8,128)(2,1)S(1)}, bf16[512,1536]{1,0:T(8,128)(2,1)}, u32[]{:S(2)}) copy-start(bf16[512,1536]{1,0:T(8,128)(2,1)} %param.11) | copy-start | bytes 4718596
  326.2 251.7 %reduce-scatter.10.cloned.1.call-start = ((), (), s32[]{:S(2)}) async-start(), calls=%async_computation.9 | async-start | bytes 20054016 | tf_op jit(solution)/shard_map/reduce_scatter | solution.py:141
  353.5 4.3 copy-start
  383.6 1.1 copy-start.4
  383.7 3.4 copy-start.9
  387.1 190.8 %copy-start.1 = (bf16[96,1536]{1,0:T(8,128)(2,1)S(1)}, bf16[96,1536]{1,0:T(8,128)(2,1)}, u32[]{:S(2)}) copy-start(bf16[96,1536]{1,0:T(8,128)(2,1)} %param.14) | copy-start | bytes 884740
Sparse Core Ops, SparseCore 0:
  16.3 54.9 all-gather.4
  78.6 41.9 reduce-scatter.5
  123.4 53.1 all-gather.8
  178.6 25.7 all-gather.6
  229.8 44.5 reduce-scatter.7
  326.3 27.1 all-gather.10
  383.8 194.0 reduce-scatter.9
where the time goes:
time: 595 us; the launch traced here: 594 us
  waiting for transfers between devices  407 us (68%)
  matrix products  89.7 us (15%)
  local copies, waits for them, and re-layouts  37.6 us (6%)
  other arithmetic  26.8 us (5%)
  blocking collectives  17.7 us (3%)
  between operations  14.3 us (2%)
    reduce_scatter x1, waiting for transfers between devices, shards(): lax.psum_scatter(jnp.concatenate((contract_first(grad_values, hidden), co...  181 us
    all_gather x1, waiting for transfers between devices, shards(): lax.all_gather(unit_v.astype(jnp.bfloat16), 'fsdp', axis=0, tiled=True)  55 us
    reduce_scatter x1, waiting for transfers between devices, shards(): lax.psum_scatter(grad_attn_parts, 'grp', scatter_dimension=1, tiled=True)  44.7 us
    all_gather x1, waiting for transfers between devices, shards(): lax.all_gather(unit_o.astype(jnp.bfloat16), 'fsdp', axis=0, tiled=True)  40.5 us
    reduce_scatter x1, waiting for transfers between devices, shards(): lax.psum_scatter(value_parts, 'grp', scatter_dimension=1, tiled=True)  39 us
    dot_general x20, matrix products, contract_last(): lax.dot_general(left, right, (((1,), (1,)), ((), ())), preferred_element_...  28.7 us
    all_gather x1, waiting for transfers between devices, shards(): attn_all = lax.all_gather(attn_mine, 'grp', axis=1, tiled=True)  27.7 us
    dot_general x14, matrix products, contract_first(): lax.dot_general(left, right, (((0,), (0,)), ((), ())), preferred_element_...  27.4 us
  transfers between devices with their start and end apart: 7, of which 7 were waited for; matrix products, arithmetic and copies ran while one was open for 6% of the time, Pallas kernels for 0%

commit v1 on v0

v1 whole, which is shorter than its diff:
```python
import jax
import jax.numpy as jnp
from jax import lax
from jax.experimental import pallas as pl
from jax.experimental.pallas import tpu as pltpu
from jax.sharding import PartitionSpec as P

D = 3072
HS = 128


EPS = 1e-06


def contract_last(left, right):
    return lax.dot_general(
        left, right, (((1,), (1,)), ((), ())), preferred_element_type=jnp.float32
    )


def contract_first(left, right):
    return lax.dot_general(
        left, right, (((0,), (0,)), ((), ())), preferred_element_type=jnp.float32
    )


def cost(flops, nbytes):
    return pl.CostEstimate(flops=flops, bytes_accessed=nbytes, transcendentals=0)


def probs_kernel(q_ref, k_ref, probs_ref):
    length = q_ref.shape[0]
    score_scale = q_ref.shape[1] ** (-0.5)
    scores = contract_last(q_ref[...], k_ref[...]) * score_scale
    row_pos = lax.broadcasted_iota(jnp.int32, (length, length), 0)
    col_pos = lax.broadcasted_iota(jnp.int32, (length, length), 1)
    scores = jnp.where(row_pos >= col_pos, scores, -1e30)
    row_peak = jnp.max(scores, axis=1, keepdims=True)
    exp_terms = jnp.exp(scores - row_peak)
    probs_ref[0] = exp_terms * (1.0 / jnp.sum(exp_terms, axis=1, keepdims=True))


def forward_kernel(probs_ref, part_ref, recv_ref, scale_ref, attn_ref, values_ref):
    values = (part_ref[...] + recv_ref[...].astype(jnp.float32)) * scale_ref[...]
    values_b = values.astype(jnp.bfloat16)
    values_ref[...] = values_b
    attn_ref[...] = jnp.dot(
        probs_ref[0].astype(jnp.bfloat16), values_b, preferred_element_type=jnp.float32
    ).astype(jnp.bfloat16)


def backward_kernel(
    probs_ref, q_ref, k_ref, v_ref, part_ref, recv_ref, gq_ref, gk_ref, gv_ref
):
    score_scale = q_ref.shape[1] ** (-0.5)
    grad_head = (part_ref[...] + recv_ref[...].astype(jnp.float32)).astype(jnp.bfloat16)
    probs = probs_ref[0]
    grad_prob = contract_last(grad_head, v_ref[...])
    row_delta = jnp.sum(probs * grad_prob, axis=1, keepdims=True)
    grad_score = (probs * (grad_prob - row_delta)).astype(jnp.bfloat16)
    gv_ref[...] = contract_first(probs.astype(jnp.bfloat16), grad_head).astype(jnp.bfloat16)
    gq_ref[...] = (
        jnp.dot(grad_score, k_ref[...], preferred_element_type=jnp.float32) * score_scale
    ).astype(jnp.bfloat16)
    gk_ref[...] = (contract_first(grad_score, q_ref[...]) * score_scale).astype(jnp.bfloat16)


def head_spec(length):
    return pl.BlockSpec((length, HS), lambda h: (0, h))


def square_spec(length):
    return pl.BlockSpec((1, length, length), lambda h: (h, 0, 0))


def head_probs(queries, keys):
    length, width = queries.shape
    heads = width // HS
    return pl.pallas_call(
        probs_kernel,
        grid=(heads,),
        in_specs=[head_spec(length)] * 2,
        out_specs=square_spec(length),
        out_shape=jax.ShapeDtypeStruct((heads, length, length), jnp.float32),
        cost_estimate=cost(heads * 30 * HS * length * length, 4 * heads * length * length),
    )(queries, keys)


def attend(probs, part, recv, scale):
    length, width = part.shape
    heads = width // HS
    one = head_spec(length)
    shape = jax.ShapeDtypeStruct((length, width), jnp.bfloat16)
    return pl.pallas_call(
        forward_kernel,
        grid=(heads,),
        in_specs=[square_spec(length), one, one, pl.BlockSpec((1, HS), lambda h: (0, h))],
        out_specs=[one, one],
        out_shape=[shape, shape],
        cost_estimate=cost(heads * 4 * HS * length * length, 6 * heads * length * length),
    )(probs, part, recv, scale)


def attend_backward(probs, queries, keys, values, part, recv):
    length, width = part.shape
    heads = width // HS
    one = head_spec(length)
    shape = jax.ShapeDtypeStruct((length, width), jnp.bfloat16)
    return pl.pallas_call(
        backward_kernel,
        grid=(heads,),
        in_specs=[square_spec(length)] + [one] * 5,
        out_specs=[one] * 3,
        out_shape=[shape] * 3,
        cost_estimate=cost(heads * 30 * HS * length * length, 6 * heads * length * length),
    )(probs, queries, keys, values, part, recv)


def shards(hidden, queries, attn_keys, w_value, w_out, alpha, out_grad):
    groups = lax.axis_size("grp")
    assert groups == 2
    me = lax.axis_index("grp")
    swap = [(0, 1), (1, 0)]

    def exchange(block):
        return lax.ppermute(block, "grp", swap)

    def mine_and_other(weight):
        rows = weight.shape[0] // groups
        return (
            lax.dynamic_slice_in_dim(weight, me * rows, rows, 0),
            lax.dynamic_slice_in_dim(weight, (1 - me) * rows, rows, 0),
        )

    def in_order(mine, other):
        return jnp.concatenate(
            (jnp.where(me == 0, mine, other), jnp.where(me == 0, other, mine)), axis=1
        )

    raw_v = lax.all_gather(w_value, "fsdp", axis=0, tiled=True)
    value_rows = w_value.astype(jnp.float32)
    out_rows = w_out.astype(jnp.float32)
    own_sums = jnp.stack(
        (jnp.sum(value_rows * value_rows, axis=1), jnp.sum(out_rows * out_rows, axis=1))
    )
    own_sums = own_sums + exchange(own_sums)
    norms = jnp.sqrt(own_sums + EPS)
    norm_v = norms[0][:, None]
    norm_o = norms[1][:, None]
    unit_v = value_rows / norm_v
    unit_o = out_rows / norm_o
    weight_o = lax.all_gather(unit_o.astype(jnp.bfloat16), "fsdp", axis=0, tiled=True)
    all_norm_v = lax.all_gather(norms[0], "fsdp", axis=0, tiled=True)
    probs = head_probs(queries, attn_keys)

    raw_mine, raw_other = mine_and_other(raw_v)
    value_recv = exchange(contract_last(hidden, raw_other).astype(jnp.bfloat16))
    value_part = contract_last(hidden, raw_mine)
    width = queries.shape[1]
    scale = 1.0 / lax.dynamic_slice_in_dim(all_norm_v, me * width, width, 0)
    attn_mine, values = attend(probs, value_part, value_recv, scale[None, :])
    weight_v = (raw_v.astype(jnp.float32) / all_norm_v[:, None]).astype(jnp.bfloat16)
    attn_all = in_order(attn_mine, exchange(attn_mine))
    proj = jnp.dot(attn_all, weight_o, preferred_element_type=jnp.float32)
    hidden_f = hidden.astype(jnp.float32)
    keep_rate = 1.0 - alpha
    grad_out = out_grad.astype(jnp.float32)
    moments = jnp.stack(
        (
            jnp.sum(proj * proj, axis=1),
            jnp.sum(keep_rate * keep_rate * hidden_f * hidden_f, axis=1),
            jnp.sum(keep_rate * alpha * hidden_f * proj, axis=1),
            jnp.sum(alpha * alpha * proj * proj, axis=1),
            jnp.sum(grad_out * keep_rate * hidden_f, axis=1),
            jnp.sum(grad_out * alpha * proj, axis=1),
        )
    )
    moments = moments + exchange(moments)
    proj_rs = lax.rsqrt(moments[0] / D + EPS)[:, None]
    cross_sum = moments[2][:, None]
    alpha_sum = moments[3][:, None]
    mix_mean = (moments[1][:, None] + 2.0 * proj_rs * cross_sum + proj_rs * proj_rs * alpha_sum) / D
    mix_rs = lax.rsqrt(mix_mean + EPS)
    mixed = hidden_f + alpha * (proj * proj_rs - hidden_f)
    new_hidden = (mixed * mix_rs).astype(jnp.bfloat16)
    grad_mean = (moments[4][:, None] + proj_rs * moments[5][:, None]) / D
    grad_mix = mix_rs * (grad_out - mixed * mix_rs * mix_rs * grad_mean)
    grad_pn = grad_mix * alpha
    proj_mean = (
        mix_rs * moments[5][:, None]
        - mix_rs * mix_rs * mix_rs * grad_mean * (cross_sum + proj_rs * alpha_sum)
    ) / D
    grad_res = grad_mix * keep_rate
    grad_proj = proj_rs * (grad_pn - proj * proj_rs * proj_rs * proj_mean)
    grad_proj_b = grad_proj.astype(jnp.bfloat16)
    out_mine, out_other = mine_and_other(weight_o)
    grad_recv = exchange(contract_last(grad_proj_b, out_other).astype(jnp.bfloat16))
    grad_part = contract_last(grad_proj_b, out_mine)
    gw_o_own = lax.psum_scatter(
        contract_first(attn_all, grad_proj_b).astype(jnp.bfloat16),
        "fsdp",
        scatter_dimension=0,
        tiled=True,
    ).astype(jnp.float32)
    grad_q, grad_k, grad_v = attend_backward(
        probs, queries, attn_keys, values, grad_part, grad_recv
    )
    grad_values = in_order(grad_v, exchange(grad_v))
    gw_v_own = lax.psum_scatter(
        contract_first(grad_values, hidden).astype(jnp.bfloat16),
        "fsdp",
        scatter_dimension=0,
        tiled=True,
    ).astype(jnp.float32)
    grad_hidden = (
        grad_res + jnp.dot(grad_values, weight_v, preferred_element_type=jnp.float32)
    ).astype(jnp.bfloat16)
    dot_o = jnp.sum(gw_o_own * unit_o, axis=1, keepdims=True)
    dot_o = dot_o + exchange(dot_o)
    grad_w_out = (gw_o_own - unit_o * dot_o) / norm_o
    dot_v = jnp.sum(gw_v_own * unit_v, axis=1, keepdims=True)
    dot_v = dot_v + exchange(dot_v)
    grad_w_value = (gw_v_own - unit_v * dot_v) / norm_v
    return (new_hidden, grad_hidden, grad_q, grad_k, grad_w_value, grad_w_out)


def solution(mesh):
    placed = (
        P("fsdp", "grp"),
        P("fsdp", "grp"),
        P("fsdp", "grp"),
        P("fsdp", "grp"),
        P("fsdp", "grp"),
        P("grp"),
        P("fsdp", "grp"),
    )
    return jax.shard_map(
        shards,
        mesh=mesh,
        in_specs=placed,
        out_specs=(
            P("fsdp", "grp"),
            P("fsdp", "grp"),
            P("fsdp", "grp"),
            P("fsdp", "grp"),
            P("fsdp", "grp"),
            P("fsdp", "grp"),
        ),
        check_vma=False,
    )
```

time: 595 us -> 331 us (0.56)
  waiting for transfers between devices: 407 us -> 186 us
  matrix products: 89.7 us -> 39.5 us
  local copies, waits for them, and re-layouts: 37.6 us -> 6.36 us
  Pallas kernels: 0 us -> 23 us
  blocking collectives: 17.7 us -> 32.5 us
  starting transfers between devices: 0.29 us -> 10.6 us
  other arithmetic: 26.8 us -> 17.7 us
    reduce_scatter x3 -> x2, waiting for transfers between devices: 265 us -> 86.7 us  [the longest x1 67.5 us: shards(): lax.psum_scatter(contract_first(grad_values, hidden).astype(jnp.bfloat16)...]
    all_gather x3 -> x1, waiting for transfers between devices: 102 us -> 49.4 us  [shards(): raw_v = lax.all_gather(w_value, 'fsdp', axis=0, tiled=True)]
    ppermute x0 -> x8, waiting for transfers between devices: none -> 49.2 us  [exchange(): return lax.ppermute(block, 'grp', swap)]
    all_gather x1, waiting for transfers between devices: 40.5 us -> 0.01 us  [shards(): lax.all_gather(unit_o.astype(jnp.bfloat16), 'fsdp', axis=0, tiled=True)]
    unnamed x0 -> x1, blocking collectives: none -> 32.5 us
    pallas_call x0 -> x3, Pallas kernels: none -> 23 us  [the longest x1 9.68 us: attend_backward(): pl.pallas_call(backward_kernel, grid=(heads,), in_specs=[square_spec(leng...]
    unnamed x37 -> x36, local copies, waits for them, and re-layouts: 26.4 us -> 5.74 us
    dot_general x14 -> x2, matrix products: 27.4 us -> 8.63 us  [contract_first(): lax.dot_general(left, right, (((0,), (0,)), ((), ())), preferred_element_...]
  transfers between devices with their start and end apart: 7 -> 12, of which waited for: 7 -> 9; matrix products, arithmetic and copies ran while one was open for 6% -> 12% of each run, Pallas kernels for 0% -> 7%
where the time goes in v1:
time: 331 us; the launch traced here: 330 us
  waiting for transfers between devices  186 us (56%)
  matrix products  39.5 us (12%)
  blocking collectives  32.5 us (10%)
  Pallas kernels  23 us (7%)
  other arithmetic  17.7 us (5%)
  between operations  14.6 us (4%)
  starting transfers between devices  10.6 us (3%)
  local copies, waits for them, and re-layouts  6.36 us (2%)
    reduce_scatter x1, waiting for transfers between devices, shards(): lax.psum_scatter(contract_first(grad_values, hidden).astype(jnp.bfloat16)...  67.5 us
    all_gather x1, waiting for transfers between devices, shards(): raw_v = lax.all_gather(w_value, 'fsdp', axis=0, tiled=True)  49.4 us
    ppermute x8, waiting for transfers between devices, exchange(): return lax.ppermute(block, 'grp', swap)  49.2 us
    unnamed x1, blocking collectives  32.5 us
    reduce_scatter x1, waiting for transfers between devices, shards(): lax.psum_scatter(contract_first(attn_all, grad_proj_b).astype(jnp.bfloat1...  19.1 us
    dot_general x4, matrix products, contract_last(): lax.dot_general(left, right, (((1,), (1,)), ((), ())), preferred_element_...  15.2 us
    ppermute x8, starting transfers between devices, exchange(): return lax.ppermute(block, 'grp', swap)  10.2 us
    pallas_call x1, Pallas kernels, attend_backward(): pl.pallas_call(backward_kernel, grid=(heads,), in_specs=[square_spec(leng...  9.68 us
  transfers between devices with their start and end apart: 12, of which 9 were waited for; matrix products, arithmetic and copies ran while one was open for 12% of the time, Pallas kernels for 7%

profile of v1, /device:TPU:0, one launch (start us, length us, event | category | flops | bytes accessed | tf_op | source)
XLA Modules:
  0.0 330.3 jit_solution(9660467459168769022)
XLA Ops:
  7.2 0.0 all-gather.4.cloned.1.call-start
  7.2 0.7 all-gather.4.cloned.1.call-update
  7.9 0.0 all-gather.6.cloned.1.call-start
  7.9 1.1 fusion.34
  9.1 1.1 fusion.35
  10.2 3.0 collective-permute-start.1
  13.3 1.6 collective-permute-done.1
  14.8 1.8 fusion.57
  16.6 0.0 all-gather.6.cloned.1.call-update
  16.7 0.0 reduce-scatter.5.cloned.1.call-start
  16.7 49.4 %all-gather.4.cloned.1.call-done = bf16[1536,1536]{1,0:T(8,128)(2,1)} async-done(((bf16[96,1536]{1,0:T(8,128)(2,1)}), bf16[1536,1536]{1,0:T(8,128)(2,1)}) %all-gather.4.cloned.1.call-update) | async-done | bytes 4718608 | tf_op jit(solution)/shard_map/all_gather | solution.py:140
  66.1 3.5 %fusion.30 = bf16[512,768]{1,0:T(8,128)(2,1)S(1)} fusion(bf16[512,1536]{1,0:T(8,128)(2,1)} %param.7, bf16[1536,1536]{1,0:T(8,128)(2,1)} %all-gather.4.cloned.1.call-done, s32[]{:T(128)S(6)} %select_n.31), kind=kOutput, calls=%fused_computation.41 | convolution fusion | flops 1208352768 | bytes 4718596 | tf_op jit(solution)/shard_map/dot_general | solution.py:16
  69.7 0.0 copy-start.15
  69.7 0.0 copy-start.4
  69.7 1.5 collective-permute-start
  71.2 6.9 %shard_map.118.probs_ref = f32[6,512,512]{2,1,0:T(8,128)} custom-call(bf16[512,768]{1,0:T(8,128)(2,1)} %q_ref.3, bf16[512,768]{1,0:T(8,128)(2,1)} %k_ref.3), custom_call_target="tpu_custom_call" | custom-call | flops 6039797760 | bytes 6291456 | tf_op jit(solution)/shard_map/pallas_call | solution.py:79
  78.1 0.6 dynamic-slice.1
  79.3 0.1 fusion.56
  79.5 32.5 %all-reduce = f32[1536]{0:T(1024)S(1)} all-reduce(f32[1536]{0:T(1024)S(1)} %fusion.56), channel_id=2, replica_groups=mesh['fsdp'=16,'grp'=2] {'fsdp'}, use_global_device_ids=true, to_apply=%add | all-reduce | flops 1536 | bytes 12288
  111.9 0.1 dynamic-slice_divide_fusion
  112.0 0.6 reshape.151.scale_ref
  112.6 4.2 %fusion.21.part_ref = f32[512,768]{1,0:T(8,128)} fusion(bf16[512,1536]{1,0:T(8,128)(2,1)S(1)} %copy-done.4, bf16[1536,1536]{1,0:T(8,128)(2,1)} %all-gather.4.cloned.1.call-done, s32[]{:T(128)S(6)} %select_n.30), kind=kOutput, calls=%fused_computation.38 | convolution fusion | flops 1207959552 | bytes 5505028 | tf_op jit(solution)/shard_map/dot_general | solution.py:16
  116.8 0.0 collective-permute-done.recv_ref
  116.8 0.9 copy-done.9
  117.7 6.5 %shard_map.119 = (bf16[512,768]{1,0:T(8,128)(2,1)}, bf16[512,768]{1,0:T(8,128)(2,1)}) custom-call(f32[6,512,512]{2,1,0:T(8,128)} %shard_map.118.probs_ref, f32[512,768]{1,0:T(8,128)} %fusion.21.part_ref, bf16[512,768]{1,0:T(8,128)(2,1)} %copy-done.9, f32[1,768]{1,0:T(1,128)} %reshape.151.scale_ref), custom_call_target="tpu_custom_call" | custom-call | flops 805306368 | bytes 9437184 | tf_op jit(solution)/shard_map/pallas_call | solution.py:94
  124.2 1.0 collective-permute-start.2
  125.2 0.0 copy-done.13
  125.2 17.4 %collective-permute-done.2 = bf16[512,768]{1,0:T(8,128)(2,1)S(1)} collective-permute-done((bf16[512,768]{1,0:T(8,128)(2,1)}, bf16[512,768]{1,0:T(8,128)(2,1)S(1)}, u32[]{:S(2)}, u32[]{:S(2)}) %collective-permute-start.2) | collective-permute-done | bytes 786464 | tf_op jit(solution)/shard_map/ppermute | solution.py:126
  142.6 2.4 broadcast_select_fusion.3
  145.0 7.5 %fusion.4 = (f32[512]{0:T(512)S(1)}, f32[512]{0:T(512)S(1)}, f32[512]{0:T(512)S(1)}, f32[512]{0:T(512)S(1)}, f32[512]{0:T(512)S(1)}, /*index=5*/f32[512]{0:T(512)S(1)}, f32[512,1536]{1,0:T(8,128)S(1)}) fusion(bf16[512,1536]{1,0:T(8,128)(2,1)} %param.13, f32[1536]{0:T(1024)S(1)} %copy-done.13, f32[1536]{0:T(1024)S(1)} %get-tuple-element.35, ...), kind=kOutput, calls=%fused_computation.17 | convolution fusion | flops 2434003968 | bytes 12625920 | tf_op jit(solution)/shard_map/dot_general | solution.py:164
  152.5 0.6 collective-permute-start.3
  153.2 3.2 collective-permute-done.3
  156.4 0.0 copy-start.10
  156.4 0.0 copy-start.11
  156.4 4.5 %multiply_convert_fusion = (bf16[512,1536]{1,0:T(8,128)(2,1)S(1)}, bf16[512,1536]{1,0:T(8,128)(2,1)}) fusion(f32[512,1536]{1,0:T(8,128)S(1)} %get-tuple-element.43, bf16[512,1536]{1,0:T(8,128)(2,1)} %param.13, f32[512]{0:T(512)S(1)} %get-tuple-element.36, f32[512]{0:T(512)S(1)} %get-tuple-element.40, f32[512]{0:T(512)S(1)} %get-tuple-element.37, ...), kind=kLoop, calls=%fused_computation.25 | loop fusion | flops 14155776 | bytes 9451520 | tf_op jit(solution)/shard_map/convert_element_type | solution.py:195
  160.9 1.1 copy-done.6
  162.0 4.3 %convolution_convert_fusion = bf16[1536,1536]{1,0:T(8,128)(2,1)} fusion(bf16[512,1536]{1,0:T(8,128)(2,1)S(1)} %get-tuple-element.22, bf16[512,768]{1,0:T(8,128)(2,1)S(1)} %copy-done.11, bf16[512,768]{1,0:T(8,128)(2,1)S(1)} %copy-done.10), kind=kOutput, calls=%fused_computation.1 | convolution fusion | flops 2421424128 | bytes 7864320 | tf_op jit(solution)/shard_map/dot_general | solution.py:22
  166.3 0.0 reduce-scatter.5.cloned.1.call-update
  166.4 0.2 reduce-scatter.3.cloned.1.call-start
  166.6 1.2 copy-done.7
  167.7 3.1 fusion.27
  170.9 0.6 collective-permute-start.4
  171.5 4.4 %fusion.15.part_ref = f32[512,768]{1,0:T(8,128)} fusion(bf16[512,1536]{1,0:T(8,128)(2,1)S(1)} %copy-done.7, bf16[1536,1536]{1,0:T(8,128)(2,1)} %all-gather.6.cloned.1.call-done, s32[]{:T(128)S(6)} %select_n.30), kind=kOutput, calls=%fused_computation.30 | convolution fusion | flops 1207959552 | bytes 5505028 | tf_op jit(solution)/shard_map/dot_general | solution.py:16
  175.8 11.3 %collective-permute-done.4.recv_ref = bf16[512,768]{1,0:T(8,128)(2,1)S(1)} collective-permute-done((bf16[512,768]{1,0:T(8,128)(2,1)S(1)}, bf16[512,768]{1,0:T(8,128)(2,1)S(1)}, u32[]{:S(2)}, u32[]{:S(2)}) %collective-permute-start.4) | collective-permute-done | bytes 786464 | tf_op jit(solution)/shard_map/ppermute | solution.py:126
  187.1 0.9 copy-done.14
  188.0 9.7 %shard_map.120 = (bf16[512,768]{1,0:T(8,128)(2,1)}, bf16[512,768]{1,0:T(8,128)(2,1)}, bf16[512,768]{1,0:T(8,128)(2,1)}) custom-call(f32[6,512,512]{2,1,0:T(8,128)} %shard_map.118.probs_ref, bf16[512,768]{1,0:T(8,128)(2,1)} %q_ref.3, bf16[512,768]{1,0:T(8,128)(2,1)} %k_ref.3, bf16[512,768]{1,0:T(8,128)(2,1)} %get-tuple-element.12.v_ref, ...), custom_call_target="tpu_custom_call" | custom-call | flops 6039797760 | bytes 9437184 | tf_op jit(solution)/shard_map/pallas_call | solution.py:109
  197.7 0.4 collective-permute-start.5
  198.1 14.8 %collective-permute-done.5 = bf16[512,768]{1,0:T(8,128)(2,1)S(1)} collective-permute-done((bf16[512,768]{1,0:T(8,128)(2,1)}, bf16[512,768]{1,0:T(8,128)(2,1)S(1)}, u32[]{:S(2)}, u32[]{:S(2)}) %collective-permute-start.5) | collective-permute-done | bytes 786464 | tf_op jit(solution)/shard_map/ppermute | solution.py:126
  212.8 1.2 broadcast_select_fusion.1
  214.1 0.9 copy-done.12
  215.0 4.3 %convolution_convert_fusion.1 = bf16[1536,1536]{1,0:T(8,128)(2,1)} fusion(bf16[512,1536]{1,0:T(8,128)(2,1)S(1)} %copy-done.5, bf16[512,768]{1,0:T(8,128)(2,1)S(1)} %get-tuple-element.25, bf16[512,768]{1,0:T(8,128)(2,1)S(1)} %get-tuple-element.24), kind=kOutput, calls=%fused_computation.2 | convolution fusion | flops 2421424128 | bytes 7864320 | tf_op jit(solution)/shard_map/dot_general | solution.py:22
  219.3 0.0 reduce-scatter.3.cloned.1.call-update
  219.3 19.1 %reduce-scatter.5.cloned.1.call-done = bf16[96,1536]{1,0:T(8,128)(2,1)} async-done(((bf16[1536,1536]{1,0:T(8,128)(2,1)}), bf16[96,1536]{1,0:T(8,128)(2,1)}) %reduce-scatter.5.cloned.1.call-update) | async-done | bytes 294928 | tf_op jit(solution)/shard_map/reduce_scatter | solution.py:199
  238.5 1.2 fusion.38
  239.7 0.0 copy-start.1
  239.7 1.5 collective-permute-start.7
  241.2 8.2 %fusion.12 = bf16[512,1536]{1,0:T(8,128)(2,1)} fusion(bf16[1536,1536]{1,0:T(8,128)(2,1)} %all-gather.4.cloned.1.call-done, f32[1536]{0:T(1024)S(1)} %all-reduce, bf16[512,1536]{1,0:T(8,128)(2,1)S(1)} %copy-done.3, f32[512]{0:T(512)S(1)} %get-tuple-element.40, f32[512]{0:T(512)S(1)} %get-tuple-element.37, f32[1536]{0:T(1024)S(1)} %get-tuple-element.38, ...), kind=kOutput, calls=%fused_computation.27 | convolution fusion | flops 2437152768 | bytes 14180352 | tf_op jit(solution)/shard_map/dot_general | solution.py:216
  249.4 0.0 collective-permute-done.7
  249.4 67.5 %reduce-scatter.3.cloned.1.call-done = bf16[96,1536]{1,0:T(8,128)(2,1)} async-done(((bf16[1536,1536]{1,0:T(8,128)(2,1)}), bf16[96,1536]{1,0:T(8,128)(2,1)}) %reduce-scatter.3.cloned.1.call-update) | async-done | bytes 294928 | tf_op jit(solution)/shard_map/reduce_scatter | solution.py:209
  317.0 1.2 fusion.36
  318.2 1.5 collective-permute-start.6
  319.7 1.0 fusion.39
  320.7 1.1 collective-permute-done.6
  321.9 2.0 fusion.37
  (33 shorter events, 0.2 us)
Async XLA Ops:
  7.2 59.0 %all-gather.4.cloned.1.call-start = ((), (), s32[]{:S(2)}) async-start(), calls=%async_computation.2 | async-start | bytes 5013504 | tf_op jit(solution)/shard_map/all_gather | solution.py:140
  7.9 137.1 %all-gather.6.cloned.1.call-start = ((), (), s32[]{:S(2)}) async-start(), calls=%async_computation.3 | async-start | bytes 5013504 | tf_op jit(solution)/shard_map/all_gather | solution.py:152
  10.2 4.6 %collective-permute-start.1 = (f32[2,96]{1,0:T(2,128)S(1)}, f32[2,96]{1,0:T(2,128)S(1)}, u32[]{:S(2)}, u32[]{:S(2)}) collective-permute-start(f32[2,96]{1,0:T(2,128)S(1)} %pad_maximum_fusion.6), channel_id=1, source_target_pairs={{0,1},{1,0},{2,3},{3,2},{4,5},{5,4},{6,7},{7,6},{8,9},{9,8},{10,11... | collective-permute-start | bytes 2312 | tf_op jit(solution)/shard_map/ppermute | solution.py:126
  16.7 221.8 %reduce-scatter.5.cloned.1.call-start = ((), (), s32[]{:S(2)}) async-start(), calls=%async_computation.5 | async-start | bytes 5013504 | tf_op jit(solution)/shard_map/reduce_scatter | solution.py:199
  69.7 8.4 %copy-start.15 = (u32[32]{0:T(128)S(1)}, u32[32]{0:T(128)}, u32[]{:S(2)}) copy-start(u32[32]{0:T(128)} %constant.33) | copy-start | bytes 388
  69.7 42.9 %copy-start.4 = (bf16[512,1536]{1,0:T(8,128)(2,1)S(1)}, bf16[512,1536]{1,0:T(8,128)(2,1)}, u32[]{:S(2)}) copy-start(bf16[512,1536]{1,0:T(8,128)(2,1)} %param.7) | copy-start | bytes 4718596
  69.7 47.1 %collective-permute-start = (bf16[512,768]{1,0:T(8,128)(2,1)S(1)}, bf16[512,768]{1,0:T(8,128)(2,1)S(1)}, u32[]{:S(2)}, u32[]{:S(2)}) collective-permute-start(bf16[512,768]{1,0:T(8,128)(2,1)S(1)} %fusion.30), channel_id=1, source_target_pairs={{0,1},{1,0},{2,3},{3,2},{4,5},{5,4},{6,7},{7,6},{8,9},{9,8},{10,11... | collective-permute-start | bytes 2359304 | tf_op jit(solution)/shard_map/ppermute | solution.py:126
  116.8 8.4 %copy-start.13 = (f32[1536]{0:T(1024)S(1)}, f32[1536]{0:T(1024)}, u32[]{:S(2)}) copy-start(f32[1536]{0:T(1024)} %param.12) | copy-start | bytes 18436
  116.8 0.9 copy-start.9
  124.2 18.4 %collective-permute-start.2 = (bf16[512,768]{1,0:T(8,128)(2,1)}, bf16[512,768]{1,0:T(8,128)(2,1)S(1)}, u32[]{:S(2)}, u32[]{:S(2)}) collective-permute-start(bf16[512,768]{1,0:T(8,128)(2,1)} %get-tuple-element.11), channel_id=1, source_target_pairs={{0,1},{1,0},{2,3},{3,2},{4,5},{5,4},{6,7},{7,6},{8,9},{9,8},{10,11... | collective-permute-start | bytes 2359304 | tf_op jit(solution)/shard_map/ppermute | solution.py:126
  152.5 8.4 %copy-start.2 = (f32[512,1536]{1,0:T(8,128)}, f32[512,1536]{1,0:T(8,128)S(1)}, u32[]{:S(2)}) copy-start(f32[512,1536]{1,0:T(8,128)S(1)} %get-tuple-element.43) | copy-start | bytes 9437188
  152.5 3.8 %collective-permute-start.3 = (f32[6,512]{1,0:T(8,128)S(1)}, f32[6,512]{1,0:T(8,128)S(1)}, u32[]{:S(2)}, u32[]{:S(2)}) collective-permute-start(f32[6,512]{1,0:T(8,128)S(1)} %stack.39), channel_id=1, source_target_pairs={{0,1},{1,0},{2,3},{3,2},{4,5},{5,4},{6,7},{7,6},{8,9},{9,8},{10,11... | collective-permute-start | bytes 36872 | tf_op jit(solution)/shard_map/ppermute | solution.py:126
  156.4 5.6 %copy-start.10 = (bf16[512,768]{1,0:T(8,128)(2,1)S(1)}, bf16[512,768]{1,0:T(8,128)(2,1)}, u32[]{:S(2)}) copy-start(bf16[512,768]{1,0:T(8,128)(2,1)} %get-tuple-element.26) | copy-start | bytes 2359300
  156.4 5.6 %copy-start.11 = (bf16[512,768]{1,0:T(8,128)(2,1)S(1)}, bf16[512,768]{1,0:T(8,128)(2,1)}, u32[]{:S(2)}) copy-start(bf16[512,768]{1,0:T(8,128)(2,1)} %get-tuple-element.27) | copy-start | bytes 2359300
  160.9 1.1 copy-start.6
  166.3 1.4 copy-start.7
  166.4 150.6 %reduce-scatter.3.cloned.1.call-start = ((), (), s32[]{:S(2)}) async-start(), calls=%async_computation.4 | async-start | bytes 5013504 | tf_op jit(solution)/shard_map/reduce_scatter | solution.py:209
  170.9 16.2 %collective-permute-start.4 = (bf16[512,768]{1,0:T(8,128)(2,1)S(1)}, bf16[512,768]{1,0:T(8,128)(2,1)S(1)}, u32[]{:S(2)}, u32[]{:S(2)}) collective-permute-start(bf16[512,768]{1,0:T(8,128)(2,1)S(1)} %fusion.27), channel_id=1, source_target_pairs={{0,1},{1,0},{2,3},{3,2},{4,5},{5,4},{6,7},{7,6},{8,9},{9,8},{10,11... | collective-permute-start | bytes 2359304 | tf_op jit(solution)/shard_map/ppermute | solution.py:126
  187.1 0.9 copy-start.14
  197.7 17.3 %copy-start.5 = (bf16[512,1536]{1,0:T(8,128)(2,1)S(1)}, bf16[512,1536]{1,0:T(8,128)(2,1)}, u32[]{:S(2)}) copy-start(bf16[512,1536]{1,0:T(8,128)(2,1)} %param.7) | copy-start | bytes 4718596
  197.7 15.2 %collective-permute-start.5 = (bf16[512,768]{1,0:T(8,128)(2,1)}, bf16[512,768]{1,0:T(8,128)(2,1)S(1)}, u32[]{:S(2)}, u32[]{:S(2)}) collective-permute-start(bf16[512,768]{1,0:T(8,128)(2,1)} %get-tuple-element.13), channel_id=1, source_target_pairs={{0,1},{1,0},{2,3},{3,2},{4,5},{5,4},{6,7},{7,6},{8,9},{9,8},{10,11... | collective-permute-start | bytes 2359304 | tf_op jit(solution)/shard_map/ppermute | solution.py:126
  214.1 0.9 copy-start.12
  219.3 19.2 %copy-start = (bf16[96,1536]{1,0:T(8,128)(2,1)S(1)}, bf16[96,1536]{1,0:T(8,128)(2,1)}, u32[]{:S(2)}) copy-start(bf16[96,1536]{1,0:T(8,128)(2,1)} %param.11) | copy-start | bytes 884740
  219.3 21.9 %copy-start.3 = (bf16[512,1536]{1,0:T(8,128)(2,1)S(1)}, bf16[512,1536]{1,0:T(8,128)(2,1)}, u32[]{:S(2)}) copy-start(bf16[512,1536]{1,0:T(8,128)(2,1)} %param.13) | copy-start | bytes 4718596
  239.7 77.3 %copy-start.1 = (bf16[96,1536]{1,0:T(8,128)(2,1)S(1)}, bf16[96,1536]{1,0:T(8,128)(2,1)}, u32[]{:S(2)}) copy-start(bf16[96,1536]{1,0:T(8,128)(2,1)} %param.10) | copy-start | bytes 884740
  239.7 80.0 %copy-start.8 = (bf16[96,1536]{1,0:T(8,128)(2,1)S(1)}, bf16[96,1536]{1,0:T(8,128)(2,1)}, u32[]{:S(2)}) copy-start(bf16[96,1536]{1,0:T(8,128)(2,1)} %reduce-scatter.5.cloned.1.call-done) | copy-start | bytes 884740
  239.7 9.7 %collective-permute-start.7 = (f32[96,1]{0,1:T(1,128)S(1)}, f32[96,1]{0,1:T(1,128)S(1)}, u32[]{:S(2)}, u32[]{:S(2)}) collective-permute-start(f32[96,1]{0,1:T(1,128)S(1)} %bitcast.58), channel_id=1, source_target_pairs={{0,1},{1,0},{2,3},{3,2},{4,5},{5,4},{6,7},{7,6},{8,9},{9,8},{10,11... | collective-permute-start | bytes 1160 | tf_op jit(solution)/shard_map/ppermute | solution.py:126
  318.2 3.6 %collective-permute-start.6 = (f32[96,1]{0,1:T(1,128)S(1)}, f32[96,1]{0,1:T(1,128)S(1)}, u32[]{:S(2)}, u32[]{:S(2)}) collective-permute-start(f32[96,1]{0,1:T(1,128)S(1)} %bitcast.59), channel_id=1, source_target_pairs={{0,1},{1,0},{2,3},{3,2},{4,5},{5,4},{6,7},{7,6},{8,9},{9,8},{10,11... | collective-permute-start | bytes 1160 | tf_op jit(solution)/shard_map/ppermute | solution.py:126
Sparse Core Ops, SparseCore 0:
  10.3 55.8 all-gather.3
  69.0 52.2 all-gather.5
  166.5 71.9 reduce-scatter.4
  242.2 74.7 reduce-scatter.2
